TPU v7x, 32 devices: a whole 2x2x4 slice. The times are simulated.
32 devices in a mesh: fem: 4 (over y, x), bem: 8 (over z, core).
Axes of the slice: x: 2, y: 2, z: 4, core: 2. Of those that a mesh axis runs over, the one named last changes fastest.
Arguments:
- fem_field: float32 [32, 64, 32, 128], P('fem', 'bem'), may hold values from -6 to 6
- fem_source: float32 [32, 64, 32, 128], P('fem', 'bem'), may hold values from -6 to 6
- reaction: float32 [32, 64, 32], P('fem', 'bem'), may hold values from 0.5 to 3
- bem_density: float32 [128, 8192], P(None, 'bem'), may hold values from -6 to 6
- bem_source: float32 [128, 8192], P(None, 'bem'), may hold values from -6 to 6
- bem_diagonal: float32 [8192], P('bem'), may hold values from 2 to 6
- near_blocks: bfloat16 [16, 48, 512, 512], P('bem', 'fem'), may hold values from -0.0390625 to 0.0390625
- near_pairs: int32 [16, 48], P('bem'), may hold values from 0 to 15, as said below
- low_left: bfloat16 [16, 32, 512], P('bem'), may hold values from -1 to 1
- low_right: bfloat16 [16, 32, 512], replicated, may hold values from -0.25 to 0.25
- centers: float32 [16, 3], replicated, may hold values from 0 to 4
- trace_cell: int32 [8192], P(('fem', 'bem')), may hold values from 0 to 2047
- trace_bank: int32 [8192, 1], P(('fem', 'bem')), may hold values from 0 to 7; in each aligned block of 256 rows (0 to 255, 256 to 511, ...) at most 32 rows name the same one
- trace_row: int32 [8192], P(('fem', 'bem')), may hold values from 0 to 1023
Outputs:
- fem_out: float32 [32, 64, 32, 128], P('fem', 'bem')
- bem_out: float32 [128, 8192], P('fem', 'bem')
Inputs may be any that keep to these rules, and one draw needn't show every extreme that they name: `trace_bank`: among the 256 slots of one device no bem index is named more than 32 times, and some device names some index exactly 32 times. Panel p's near-field source panels are held by bem indices within two of p's own, counted around the bem axis: near_pairs[p, k] // 2 - p // 2 is -2, -1, 0, 1 or 2 modulo 8.
All inputs are finite; a program needn't handle non-finite values.
Results may differ from a plain program's by a relative error of at most 0.0028.
Values may be sent and summed in bfloat16 or wider, within the bound.
A program may use at most 128 MiB of HBM per device.

v0:
```python
import functools

import jax
import jax.numpy as jnp
from jax import lax
from jax.experimental import pallas as pl
from jax.experimental.pallas import tpu as pltpu
from jax.sharding import PartitionSpec as P

CAP = 32
ITERS = 3


HIGHEST = lax.Precision.HIGHEST
MESH = pl.DeviceIdType.MESH


def exchange_kernel(plan, count, *refs):
    items = len(plan)
    sources, targets = refs[:items], refs[items : 2 * items]
    send_sem, recv_sem, own_sem = refs[2 * items :]
    sizes = {axis: lax.axis_size(axis) for axis in ("fem", "bem")}
    ranks = {axis: lax.axis_index(axis) for axis in ("fem", "bem")}

    def device(axis, step):
        place = dict(ranks)
        place[axis] = lax.rem(ranks[axis] + step, sizes[axis])
        return (place["fem"], place["bem"])

    def steps(kind, axis):
        return [kind % sizes[axis]] if isinstance(kind, int) else range(1, sizes[axis])

    peers = sorted({(axis, step) for kind, axis in plan for step in steps(kind, axis)})
    barrier = pltpu.get_barrier_semaphore()
    for axis, step in peers:
        pl.semaphore_signal(barrier, inc=1, device_id=device(axis, step), device_id_type=MESH)
    pl.semaphore_wait(barrier, len(peers))

    def own_place(kind, axis, source, target):
        rank = ranks[axis]
        if kind == "gather":
            rows = source.shape[1]
            return target.at[:, pl.ds(pl.multiple_of(rank * rows, rows), rows), :]
        return target.at[rank] if kind == "scatter" else target

    copies = []
    for (kind, axis), source, target in zip(plan, sources, targets):
        for step in steps(kind, axis):
            place = device(axis, step)
            there = place[0] if axis == "fem" else place[1]
            slot = len(copies)
            copy = pltpu.make_async_remote_copy(
                src_ref=source.at[there] if kind == "scatter" else source,
                dst_ref=own_place(kind, axis, source, target),
                send_sem=send_sem.at[slot],
                recv_sem=recv_sem.at[slot],
                device_id=place,
                device_id_type=MESH,
            )
            copy.start()
            copies.append(copy)
    for item, ((kind, axis), source, target) in enumerate(zip(plan, sources, targets)):
        if not isinstance(kind, int):
            copy = pltpu.make_async_copy(
                source.at[ranks[axis]] if kind == "scatter" else source,
                own_place(kind, axis, source, target),
                own_sem.at[item],
            )
            copy.start()
            copies.append(copy)
    for copy in copies:
        copy.wait()


def exchange(plan, arrays, name, collective_id):
    shapes, count = [], 0
    for (kind, axis), x in zip(plan, arrays):
        size = lax.axis_size(axis)
        count += 1 if isinstance(kind, int) else size - 1
        shape = (x.shape[0], x.shape[1] * size, x.shape[2]) if kind == "gather" else x.shape
        shapes.append(jax.ShapeDtypeStruct(shape, x.dtype))
    return pl.pallas_call(
        functools.partial(exchange_kernel, plan, count),
        out_shape=shapes,
        in_specs=[pl.BlockSpec(memory_space=pltpu.VMEM)] * len(arrays),
        out_specs=[pl.BlockSpec(memory_space=pltpu.VMEM)] * len(arrays),
        scratch_shapes=[
            pltpu.SemaphoreType.DMA((count,)),
            pltpu.SemaphoreType.DMA((count,)),
            pltpu.SemaphoreType.DMA((len(plan),)),
        ],
        cost_estimate=pl.CostEstimate(
            flops=1 << 29, bytes_accessed=sum(x.size for x in arrays) * 4, transcendentals=0
        ),
        compiler_params=pltpu.CompilerParams(
            collective_id=collective_id, has_side_effects=True, vmem_limit_bytes=8 << 20
        ),
        name=name,
    )(*arrays)


def end_faces(state):
    narrow = lambda x: x.astype(jnp.bfloat16)
    return [narrow(state[-1:]), narrow(state[:1]), narrow(state[:, -1:]), narrow(state[:, :1])]


FACE_PLAN = ((1, "fem"), (-1, "fem"), (1, "bem"), (-1, "bem"))


def neighbour_sum(state, before_x, after_x, before_y, after_y):
    wide_x = jnp.concatenate(
        [before_x.astype(jnp.float32), state, after_x.astype(jnp.float32)], axis=0
    )
    wide_y = jnp.concatenate(
        [before_y.astype(jnp.float32), state, after_y.astype(jnp.float32)], axis=1
    )
    wide_z = jnp.pad(state, ((0, 0), (0, 0), (1, 1), (0, 0)))
    beside = wide_x[2:] + wide_x[:-2] + wide_y[:, 2:] + wide_y[:, :-2]
    return beside + wide_z[:, :, 2:] + wide_z[:, :, :-2]


def near_kernel(pairs_ref, x_ref, blocks_ref, init_ref, out_ref, acc_ref):
    p, k = pl.program_id(0), pl.program_id(1)

    @pl.when(k == 0)
    def _():
        acc_ref[...] = init_ref[...]

    width = blocks_ref.shape[1]
    acc = acc_ref[...]
    for i in range(width):
        acc += jnp.dot(
            x_ref[pairs_ref[p, k * width + i]],
            blocks_ref[0, i],
            preferred_element_type=jnp.float32,
        )
    acc_ref[...] = acc

    @pl.when(k == pl.num_programs(1) - 1)
    def _():
        out_ref[...] = acc_ref[...].astype(out_ref.dtype)


def near_apply(pairs, x, blocks, init):
    panels, group, rows, cols = blocks.shape
    exc = x.shape[1]
    width = next(w for w in (4, 3, 2, 1) if group % w == 0)
    return pl.pallas_call(
        near_kernel,
        out_shape=jax.ShapeDtypeStruct((exc, panels * cols), jnp.bfloat16),
        grid_spec=pltpu.PrefetchScalarGridSpec(
            num_scalar_prefetch=1,
            grid=(panels, group // width),
            in_specs=[
                pl.BlockSpec(x.shape, lambda p, k, pairs: (0, 0, 0)),
                pl.BlockSpec((1, width, rows, cols), lambda p, k, pairs: (p, k, 0, 0)),
                pl.BlockSpec((exc, cols), lambda p, k, pairs: (0, p)),
            ],
            out_specs=pl.BlockSpec((exc, cols), lambda p, k, pairs: (0, p)),
            scratch_shapes=[pltpu.VMEM((exc, cols), jnp.float32)],
        ),
        cost_estimate=pl.CostEstimate(
            flops=2 * exc * blocks.size, bytes_accessed=2 * blocks.size, transcendentals=0
        ),
        compiler_params=pltpu.CompilerParams(
            dimension_semantics=("arbitrary", "arbitrary"), vmem_limit_bytes=52 << 20
        ),
        name="near",
    )(pairs, x, blocks, init)


def pick_kernel(node_ref, x_ref, out_ref):
    panels, exc, rows = x_ref.shape
    slots = node_ref.shape[1]
    node = node_ref[...]
    places = lax.broadcasted_iota(jnp.int32, (rows, slots), 0)

    def step(q, acc):
        hot = jnp.where(places == node - q * rows, 1.0, 0.0).astype(jnp.bfloat16)
        return acc + jnp.dot(x_ref[q], hot, preferred_element_type=jnp.float32)

    acc = lax.fori_loop(0, panels, step, jnp.zeros((exc, slots), jnp.float32), unroll=2)
    out_ref[...] = acc.astype(out_ref.dtype)


def pick_nodes(node, x):
    slots = node.shape[1]
    return pl.pallas_call(
        pick_kernel,
        out_shape=jax.ShapeDtypeStruct((x.shape[1], slots), jnp.bfloat16),
        cost_estimate=pl.CostEstimate(
            flops=2 * slots * x.size, bytes_accessed=2 * x.size, transcendentals=0
        ),
        compiler_params=pltpu.CompilerParams(vmem_limit_bytes=24 << 20),
        name="pick",
    )(node, x)


def shards(
    fem_field,
    fem_source,
    reaction,
    bem_density,
    bem_source,
    bem_diagonal,
    near_blocks,
    near_pairs,
    low_left,
    low_right,
    centers,
    trace_cell,
    trace_bank,
    trace_row,
):
    fem_count = lax.axis_size("fem")
    bem_count = lax.axis_size("bem")
    fem_rank = lax.axis_index("fem")
    bem_rank = lax.axis_index("bem")
    excitations, local_rows = bem_density.shape
    share_cols = excitations // fem_count
    local_panels = near_blocks.shape[0]
    group_size = near_blocks.shape[1]
    panel_rows = near_blocks.shape[2]
    panel_total = low_right.shape[0]
    cell_total = reaction.size
    slot_total = trace_cell.shape[0]
    first_col = fem_rank * share_cols
    slot_bank = trace_bank[:, 0]
    positions = jnp.arange(slot_total, dtype=jnp.int32)
    earlier = (slot_bank[:, None] == slot_bank[None, :]) & (positions[None, :] < positions[:, None])
    slot_place = jnp.sum(earlier.astype(jnp.int32), axis=1)
    destination = slot_bank * CAP + slot_place
    places = jnp.arange(bem_count * CAP, dtype=jnp.int32)[:, None] == destination[None, :]
    send_rows = jnp.sum(jnp.where(places, trace_row[None, :] + 1, 0), axis=1) - 1
    send_cell = jnp.sum(jnp.where(places, trace_cell[None, :] + 1, 0), axis=1) - 1
    rows_wide = jnp.full((bem_count, 8, 128), -1, jnp.int32)
    rows_wide = rows_wide.at[:, :, :CAP].set(send_rows.reshape(bem_count, 1, CAP))
    cell_ids = jnp.arange(cell_total, dtype=jnp.int32)
    send_hot = (send_cell[:, None] == cell_ids[None, :]).astype(jnp.bfloat16)
    cell_hot = (cell_ids[:, None] == trace_cell[None, :]).astype(jnp.bfloat16)
    row_ids = jnp.arange(local_rows, dtype=jnp.int32)
    node = (slot_bank * local_rows + trace_row)[None, :]
    own_first = bem_rank * local_panels
    own_centers = lax.dynamic_slice_in_dim(centers, own_first, local_panels, 0)
    offsets = own_centers[:, None, :] - centers[None, :, :]
    kernel_rows = 1.0 / (1.0 + jnp.sum(offsets * offsets, axis=-1))
    panel_ids = jnp.arange(panel_total, dtype=jnp.int32)
    own_ids = own_first + jnp.arange(local_panels, dtype=jnp.int32)
    listed = jnp.any(near_pairs[:, :, None] == panel_ids[None, None, :], axis=1)
    listed = listed | (own_ids[:, None] == panel_ids[None, :])
    kernel_rows = jnp.where(listed, 0.0, kernel_rows)
    left_wide = low_left.astype(jnp.float32)
    pair_group = lax.dynamic_slice_in_dim(near_pairs, fem_rank * group_size, group_size, 1)
    density = lax.dynamic_slice_in_dim(bem_density, first_col, share_cols, 0)
    source_part = lax.dynamic_slice_in_dim(bem_source, first_col, share_cols, 0)
    diag_row = bem_diagonal[None, :]
    fem_state = fem_field
    for sweep in range(ITERS):
        whole = bem_density if sweep == 0 else density
        narrow = whole.astype(jnp.bfloat16).reshape(-1, local_panels, panel_rows)
        narrow = jnp.transpose(narrow, (1, 0, 2))
        if sweep > 0:
            (narrow,) = exchange((("gather", "fem"),), [narrow], "share_gather", 1)
        x = lax.all_gather(narrow, "bem", axis=0, tiled=True)
        outgoing = jnp.dot(
            send_hot,
            fem_state.astype(jnp.bfloat16).reshape(cell_total, excitations),
            preferred_element_type=jnp.float32,
        ).astype(jnp.bfloat16)
        arrays = [*end_faces(fem_state), outgoing.reshape(bem_count, CAP, excitations)]
        plan = (*FACE_PLAN, ("scatter", "bem"))
        if sweep == 0:
            *layers, incoming, recv_rows = exchange(
                (*plan, ("scatter", "bem")), [*arrays, rows_wide], "first_exchange", 0
            )
            recv_rows = recv_rows[:, 0, :CAP].reshape(-1)
            recv_hot = (recv_rows[:, None] == row_ids[None, :]).astype(jnp.bfloat16)
        else:
            *layers, incoming = exchange(plan, arrays, "layer_exchange", 2)
        inside = (fem_rank > 0, fem_rank < fem_count - 1, bem_rank > 0, bem_rank < bem_count - 1)
        layers = [
            jnp.where(here, x, jnp.zeros_like(x)) for here, x in zip(inside, layers)
        ]
        traced = lax.dot_general(
            incoming.reshape(-1, excitations),
            recv_hot,
            (((0,), (0,)), ((), ())),
            preferred_element_type=jnp.float32,
        )
        partial_sum = near_apply(pair_group, x, near_blocks, traced)
        (parts,) = exchange(
            (("scatter", "fem"),),
            [partial_sum.reshape(fem_count, share_cols, local_rows)],
            "part_scatter",
            3,
        )
        own_cols = lax.dynamic_slice_in_dim(x, first_col, share_cols, 1)
        reduced = jnp.einsum(
            "qen,qrn->qer", own_cols, low_right, preferred_element_type=jnp.float32
        ).astype(jnp.bfloat16)
        reduced = lax.optimization_barrier(reduced).astype(jnp.float32)
        weights = jnp.einsum("pq,qer->per", kernel_rows, reduced, precision=HIGHEST)
        distant = jnp.einsum("per,prn->epn", weights, left_wide, precision=HIGHEST).reshape(
            share_cols, local_rows
        )
        values = pick_nodes(node, x)
        coupled = lax.dot_general(
            cell_hot, values, (((1,), (1,)), ((), ())), preferred_element_type=jnp.float32
        ).reshape(fem_state.shape)
        scale = (6.0 + reaction)[..., None]
        beside = neighbour_sum(fem_state, *layers)
        fem_next = fem_state + (fem_source - (scale * fem_state - beside) - coupled) / scale
        applied = distant + jnp.sum(parts.astype(jnp.float32), axis=0)
        density = density + (source_part - applied) / diag_row
        fem_state = fem_next
    return (fem_state, density)


def solution(mesh):
    return jax.shard_map(
        shards,
        mesh=mesh,
        in_specs=(
            P("fem", "bem", None, None),
            P("fem", "bem", None, None),
            P("fem", "bem", None),
            P(None, "bem"),
            P(None, "bem"),
            P("bem"),
            P("bem", "fem", None, None),
            P("bem", None),
            P("bem", None, None),
            P(),
            P(),
            P(("fem", "bem")),
            P(("fem", "bem"), None),
            P(("fem", "bem")),
        ),
        out_specs=(P("fem", "bem", None, None), P("fem", "bem")),
        check_vma=False,
    )
```

profile of v0, /device:TPU:0, one launch (start us, length us, event | category | flops | bytes accessed | tf_op | source)
XLA Modules:
  0.0 178.8 jit_solution(7080492815570011900)
XLA Ops:
  7.3 1.3 copy.42
  10.7 11.2 %first_exchange.1 = (bf16[1,8,32,128]{3,2,1,0:T(8,128)(2,1)S(1)}, bf16[1,8,32,128]{3,2,1,0:T(8,128)(2,1)S(1)}, bf16[8,1,32,128]{3,2,1,0:T(8,128)(2,1)S(1)}, bf16...) custom-call(bf16[1,8,32,128]{3,2,1,0:T(8,128)(2,1)S(1)} %get-tuple-element.67.refs_0_, ...), custom_call_target="tpu_custom_call" | custom-call | flops 536870912 | bytes 688128 | tf_op jit(solution)/shard_map/first_exchange/pallas_call | solution.py:82
  22.7 19.5 %all-gather.4.cloned.1.call-done.x_ref = bf16[16,128,512]{2,1,0:T(8,128)(2,1)} async-done(((bf16[2,128,512]{2,1,0:T(8,128)(2,1)}), bf16[16,128,512]{2,1,0:T(8,128)(2,1)}) %all-gather.4.cloned.1.call-update) | async-done | bytes 2097168 | tf_op jit(solution)/shard_map/all_gather | solution.py:264
  42.2 8.4 %near.3 = bf16[128,1024]{1,0:T(8,128)(2,1)S(1)} custom-call(s32[2,12]{1,0:T(2,128)S(1)} %constant_dynamic-slice_fusion.pairs_ref, bf16[16,128,512]{2,1,0:T(8,128)(2,1)} %all-gather.4.cloned.1.call-done.x_ref, bf16[2,12,512,512]{3,2,1,0:T(8,128)(2,1)} %blocks_ref.5, f32[128,1024]{1,0:T(8,128)S(1)} %fusion.41.init_ref), custom_call_target="tpu_custom_call" | custom-call | flops 1610612736 | bytes 12582912 | tf_op jit(solution)/shard_map/near/pallas_call | solution.py:148
  50.6 6.6 %part_scatter.3 = bf16[4,32,1024]{2,1,0:T(8,128)(2,1)S(1)} custom-call(bf16[4,32,1024]{2,1,0:T(8,128)(2,1)S(1)} %bitcast.69), custom_call_target="tpu_custom_call" | custom-call | flops 536870912 | bytes 524288 | tf_op jit(solution)/shard_map/part_scatter/pallas_call | solution.py:82
  58.1 1.0 fusion.76
  59.1 7.0 %share_gather.2 = bf16[2,128,512]{2,1,0:T(8,128)(2,1)} custom-call(bf16[2,32,512]{2,1,0:T(8,128)(2,1)S(1)} %bitcast.74), custom_call_target="tpu_custom_call" | custom-call | flops 536870912 | bytes 131072 | tf_op jit(solution)/shard_map/share_gather/pallas_call | solution.py:82
  66.4 2.0 %pick.3 = bf16[128,256]{1,0:T(8,128)(2,1)S(1)} custom-call(s32[1,256]{1,0:T(1,128)S(1)} %bitcast.76, bf16[16,128,512]{2,1,0:T(8,128)(2,1)S(1)} %copy-done.1), custom_call_target="tpu_custom_call" | custom-call | flops 536870912 | bytes 2097152 | tf_op jit(solution)/shard_map/pick/pallas_call | solution.py:188
  68.8 2.1 %fusion.74 = (bf16[8,8,32,128]{3,2,1,0:T(8,128)(2,1)S(1)}, f32[8,8,32,128]{3,2,1,0:T(8,128)}) fusion(f32[8,8,32,128]{3,2,1,0:T(8,128)S(1)} %copy-done.9, f32[8,8,32,128]{3,2,1,0:T(8,128)S(1)} %bitcast.83, f32[8,8,32,128]{3,2,1,0:T(8,128)S(1)} %copy-done.4, f32[8,1,32,128]{3,2,1,0:T(8,128)S(1)} %select_convert_fusion.8, ...), kind=kLoop, calls=%fused_computation.139 | loop fusion | flops 4194304 | bytes 5251072 | tf_op jit(solution)/shard_map/convert.7
  71.5 10.4 %layer_exchange.2 = (bf16[1,8,32,128]{3,2,1,0:T(8,128)(2,1)S(1)}, bf16[1,8,32,128]{3,2,1,0:T(8,128)(2,1)S(1)}, bf16[8,1,32,128]{3,2,1,0:T(8,128)(2,1)S(1)}, bf16...) custom-call(bf16[1,8,32,128]{3,2,1,0:T(8,128)(2,1)S(1)} %get-tuple-element.63.refs_0_, ...), custom_call_target="tpu_custom_call" | custom-call | flops 536870912 | bytes 655360 | tf_op jit(solution)/shard_map/layer_exchange/pallas_call | solution.py:82
  82.2 15.0 %all-gather.6.cloned.1.call-done.x_ref = bf16[16,128,512]{2,1,0:T(8,128)(2,1)} async-done(((bf16[2,128,512]{2,1,0:T(8,128)(2,1)}), bf16[16,128,512]{2,1,0:T(8,128)(2,1)}) %all-gather.6.cloned.1.call-update) | async-done | bytes 2097168 | tf_op jit(solution)/shard_map/all_gather | solution.py:264
  97.2 8.4 %near.4 = bf16[128,1024]{1,0:T(8,128)(2,1)S(1)} custom-call(s32[2,12]{1,0:T(2,128)S(1)} %constant_dynamic-slice_fusion.pairs_ref, bf16[16,128,512]{2,1,0:T(8,128)(2,1)} %all-gather.6.cloned.1.call-done.x_ref, bf16[2,12,512,512]{3,2,1,0:T(8,128)(2,1)} %blocks_ref.5, f32[128,1024]{1,0:T(8,128)S(1)} %fusion.40.init_ref), custom_call_target="tpu_custom_call" | custom-call | flops 1610612736 | bytes 12582912 | tf_op jit(solution)/shard_map/near/pallas_call | solution.py:148
  105.6 6.2 %part_scatter.4 = bf16[4,32,1024]{2,1,0:T(8,128)(2,1)S(1)} custom-call(bf16[4,32,1024]{2,1,0:T(8,128)(2,1)S(1)} %bitcast.70), custom_call_target="tpu_custom_call" | custom-call | flops 536870912 | bytes 524288 | tf_op jit(solution)/shard_map/part_scatter/pallas_call | solution.py:82
  112.7 1.0 fusion.73
  113.7 6.7 %share_gather.3 = bf16[2,128,512]{2,1,0:T(8,128)(2,1)} custom-call(bf16[2,32,512]{2,1,0:T(8,128)(2,1)S(1)} %bitcast.75), custom_call_target="tpu_custom_call" | custom-call | flops 536870912 | bytes 131072 | tf_op jit(solution)/shard_map/share_gather/pallas_call | solution.py:82
  120.5 2.0 %pick.4 = bf16[128,256]{1,0:T(8,128)(2,1)S(1)} custom-call(s32[1,256]{1,0:T(1,128)S(1)} %bitcast.77, bf16[16,128,512]{2,1,0:T(8,128)(2,1)S(1)} %copy-done.2), custom_call_target="tpu_custom_call" | custom-call | flops 536870912 | bytes 2097152 | tf_op jit(solution)/shard_map/pick/pallas_call | solution.py:188
  122.9 1.3 fusion.71
  124.8 7.5 %layer_exchange.3 = (bf16[1,8,32,128]{3,2,1,0:T(8,128)(2,1)S(1)}, bf16[1,8,32,128]{3,2,1,0:T(8,128)(2,1)S(1)}, bf16[8,1,32,128]{3,2,1,0:T(8,128)(2,1)S(1)}, bf16...) custom-call(bf16[1,8,32,128]{3,2,1,0:T(8,128)(2,1)S(1)} %get-tuple-element.59.refs_0_, ...), custom_call_target="tpu_custom_call" | custom-call | flops 536870912 | bytes 655360 | tf_op jit(solution)/shard_map/layer_exchange/pallas_call | solution.py:82
  132.8 17.3 %all-gather.8.cloned.1.call-done.x_ref = bf16[16,128,512]{2,1,0:T(8,128)(2,1)} async-done(((bf16[2,128,512]{2,1,0:T(8,128)(2,1)}), bf16[16,128,512]{2,1,0:T(8,128)(2,1)}) %all-gather.8.cloned.1.call-update) | async-done | bytes 2097168 | tf_op jit(solution)/shard_map/all_gather | solution.py:264
  150.2 8.4 %near.5 = bf16[128,1024]{1,0:T(8,128)(2,1)S(1)} custom-call(s32[2,12]{1,0:T(2,128)S(1)} %constant_dynamic-slice_fusion.pairs_ref, bf16[16,128,512]{2,1,0:T(8,128)(2,1)} %all-gather.8.cloned.1.call-done.x_ref, bf16[2,12,512,512]{3,2,1,0:T(8,128)(2,1)} %blocks_ref.5, f32[128,1024]{1,0:T(8,128)S(1)} %fusion.39.init_ref), custom_call_target="tpu_custom_call" | custom-call | flops 1610612736 | bytes 12582912 | tf_op jit(solution)/shard_map/near/pallas_call | solution.py:148
  158.5 6.6 %part_scatter.5 = bf16[4,32,1024]{2,1,0:T(8,128)(2,1)S(1)} custom-call(bf16[4,32,1024]{2,1,0:T(8,128)(2,1)S(1)} %bitcast.68), custom_call_target="tpu_custom_call" | custom-call | flops 536870912 | bytes 524288 | tf_op jit(solution)/shard_map/part_scatter/pallas_call | solution.py:82
  166.0 2.0 %pick.5 = bf16[128,256]{1,0:T(8,128)(2,1)S(1)} custom-call(s32[1,256]{1,0:T(1,128)S(1)} %bitcast.78, bf16[16,128,512]{2,1,0:T(8,128)(2,1)S(1)} %copy-done.3), custom_call_target="tpu_custom_call" | custom-call | flops 536870912 | bytes 2097152 | tf_op jit(solution)/shard_map/pick/pallas_call | solution.py:188
  168.5 1.6 divide_add_fusion
  170.1 2.2 %fusion.29 = f32[8,8,32,128]{3,2,1,0:T(8,128)} fusion(f32[8,8,32,128]{3,2,1,0:T(8,128)S(1)} %get-tuple-element.49, f32[8,8,32,128]{3,2,1,0:T(8,128)S(1)} %bitcast.84, f32[8,8,32,128]{3,2,1,0:T(8,128)S(1)} %copy-done.6, f32[8,1,32,128]{3,2,1,0:T(8,128)S(1)} %select_convert_fusion, f32[8,1,32,128]{3,2,1,0:T(8,128)S(1)} %select_convert_fusion.1, ...), kind=kLoop, calls=%fused_computation.43 | loop fusion | flops 3932160 | bytes 4726784 | tf_op jit(solution)/shard_map/add | solution.py:312
  (104 shorter events, 8.7 us)
Async XLA Ops:
  7.2 50.1 %copy-start = (bf16[16,32,512]{2,1,0:T(8,128)(2,1)S(1)}, bf16[16,32,512]{2,1,0:T(8,128)(2,1)}, u32[]{:S(2)}) copy-start(bf16[16,32,512]{2,1,0:T(8,128)(2,1)} %param.25) | copy-start | bytes 1572868
  7.2 2.3 %copy-start.8 = (f32[8,8,32,128]{3,2,1,0:T(8,128)S(1)}, f32[8,8,32,128]{3,2,1,0:T(8,128)}, u32[]{:S(2)}) copy-start(f32[8,8,32,128]{3,2,1,0:T(8,128)} %param.16) | copy-start | bytes 3145732
  7.2 2.5 %copy-start.14 = (s32[256,1]{0,1:T(1,128)S(1)}, s32[256,1]{0,1:T(1,128)}, u32[]{:S(2)}) copy-start(s32[256,1]{0,1:T(1,128)} %param.28) | copy-start | bytes 3076
  7.2 2.6 %copy-start.13 = (s32[256]{0:T(256)S(1)}, s32[256]{0:T(256)}, u32[]{:S(2)}) copy-start(s32[256]{0:T(256)} %param.27) | copy-start | bytes 3076
  7.2 2.6 %copy-start.17 = (s32[256]{0:T(256)S(1)}, s32[256]{0:T(256)}, u32[]{:S(2)}) copy-start(s32[256]{0:T(256)} %param.29) | copy-start | bytes 3076
  7.2 35.0 %all-gather.4.cloned.1.call-start = ((), (), s32[]{:S(2)}) async-start(), calls=%async_computation | async-start | bytes 2359296 | tf_op jit(solution)/shard_map/all_gather | solution.py:264
  9.5 87.8 %all-gather.6.cloned.1.call-start = ((), (), s32[]{:S(2)}) async-start(), calls=%async_computation.1 | async-start | bytes 2359296 | tf_op jit(solution)/shard_map/all_gather | solution.py:264
  9.6 12.4 %copy-start.16 = (s32[2,48]{1,0:T(2,128)S(1)}, s32[2,48]{1,0:T(2,128)}, u32[]{:S(2)}) copy-start(s32[2,48]{1,0:T(2,128)} %param.23) | copy-start | bytes 1156
  9.6 12.4 %copy-start.15 = (f32[16,3]{0,1:T(4,128)S(1)}, f32[16,3]{0,1:T(4,128)}, u32[]{:S(2)}) copy-start(f32[16,3]{0,1:T(4,128)} %param.26) | copy-start | bytes 580
  50.6 6.7 %copy-start.1 = (bf16[16,128,512]{2,1,0:T(8,128)(2,1)S(1)}, bf16[16,128,512]{2,1,0:T(8,128)(2,1)}, u32[]{:S(2)}) copy-start(bf16[16,128,512]{2,1,0:T(8,128)(2,1)} %all-gather.4.cloned.1.call-done.x_ref) | copy-start | bytes 6291460
  50.6 7.2 %copy-start.10 = (bf16[2,32,512]{2,1,0:T(8,128)(2,1)S(1)}, bf16[2,32,512]{2,1,0:T(8,128)(2,1)}, u32[]{:S(2)}) copy-start(bf16[2,32,512]{2,1,0:T(8,128)(2,1)} %param.24) | copy-start | bytes 196612
  50.6 7.4 %copy-start.11 = (f32[1024]{0:T(1024)S(1)}, f32[1024]{0:T(1024)}, u32[]{:S(2)}) copy-start(f32[1024]{0:T(1024)} %param.21) | copy-start | bytes 12292
  57.6 8.7 %copy-start.12 = (f32[8,8,32]{2,1,0:T(8,128)S(1)}, f32[8,8,32]{2,1,0:T(8,128)}, u32[]{:S(2)}) copy-start(f32[8,8,32]{2,1,0:T(8,128)} %param.18) | copy-start | bytes 24580
  66.2 84.0 %all-gather.8.cloned.1.call-start = ((), (), s32[]{:S(2)}) async-start(), calls=%async_computation.2 | async-start | bytes 2359296 | tf_op jit(solution)/shard_map/all_gather | solution.py:264
  66.2 2.6 %copy-start.4 = (f32[8,8,32,128]{3,2,1,0:T(8,128)S(1)}, f32[8,8,32,128]{3,2,1,0:T(8,128)}, u32[]{:S(2)}) copy-start(f32[8,8,32,128]{3,2,1,0:T(8,128)} %param.17) | copy-start | bytes 3145732
  66.2 2.6 %copy-start.9 = (f32[8,8,32,128]{3,2,1,0:T(8,128)S(1)}, f32[8,8,32,128]{3,2,1,0:T(8,128)}, u32[]{:S(2)}) copy-start(f32[8,8,32,128]{3,2,1,0:T(8,128)} %param.16) | copy-start | bytes 3145732
  105.6 6.3 %copy-start.2 = (bf16[16,128,512]{2,1,0:T(8,128)(2,1)S(1)}, bf16[16,128,512]{2,1,0:T(8,128)(2,1)}, u32[]{:S(2)}) copy-start(bf16[16,128,512]{2,1,0:T(8,128)(2,1)} %all-gather.6.cloned.1.call-done.x_ref) | copy-start | bytes 6291460
  120.4 2.6 %copy-start.5 = (f32[8,8,32,128]{3,2,1,0:T(8,128)S(1)}, f32[8,8,32,128]{3,2,1,0:T(8,128)}, u32[]{:S(2)}) copy-start(f32[8,8,32,128]{3,2,1,0:T(8,128)} %param.17) | copy-start | bytes 3145732
  120.4 2.6 %copy-start.7 = (f32[8,8,32,128]{3,2,1,0:T(8,128)S(1)}, f32[8,8,32,128]{3,2,1,0:T(8,128)}, u32[]{:S(2)}) copy-start(f32[8,8,32,128]{3,2,1,0:T(8,128)} %get-tuple-element.53) | copy-start | bytes 3145732
  158.5 6.7 %copy-start.3 = (bf16[16,128,512]{2,1,0:T(8,128)(2,1)S(1)}, bf16[16,128,512]{2,1,0:T(8,128)(2,1)}, u32[]{:S(2)}) copy-start(bf16[16,128,512]{2,1,0:T(8,128)(2,1)} %all-gather.8.cloned.1.call-done.x_ref) | copy-start | bytes 6291460
  166.0 4.1 %copy-start.6 = (f32[8,8,32,128]{3,2,1,0:T(8,128)S(1)}, f32[8,8,32,128]{3,2,1,0:T(8,128)}, u32[]{:S(2)}) copy-start(f32[8,8,32,128]{3,2,1,0:T(8,128)} %param.17) | copy-start | bytes 3145732
Sparse Core Ops, SparseCore 0:
  10.2 31.9 all-gather.3
  66.3 30.8 all-gather.5
  120.5 29.6 all-gather.7
where the time goes:
time: 179 us
  Pallas kernels  93.2 us (52%)
  waiting for transfers between devices  51.8 us (29%)
  between operations  14.5 us (8%)
  other arithmetic  10.2 us (6%)
  matrix products  6.22 us (3%)
  local copies, waits for them, and re-layouts  2.71 us (2%)
    pallas_call x8, Pallas kernels, exchange(): pl.pallas_call(functools.partial(exchange_kernel, plan, count), out_shape...  62.2 us
    all_gather x3, waiting for transfers between devices, shards(): x = lax.all_gather(narrow, 'bem', axis=0, tiled=True)  51.8 us
    pallas_call x3, Pallas kernels, near_apply(): pl.pallas_call(near_kernel, out_shape=jax.ShapeDtypeStruct((exc, panels *...  25.1 us
    pallas_call x3, Pallas kernels, pick_nodes(): pl.pallas_call(pick_kernel, out_shape=jax.ShapeDtypeStruct((x.shape[1], s...  5.9 us
  transfers between devices with their start and end apart: 3, of which 3 were waited for; matrix products, arithmetic and copies ran while one was open for 5% of the time, Pallas kernels for 18%

commit v1 on v0

v1 whole, which is shorter than its diff:
```python
import functools

import jax
import jax.numpy as jnp
from jax import lax
from jax.experimental import pallas as pl
from jax.experimental.pallas import tpu as pltpu
from jax.sharding import PartitionSpec as P

CAP = 32
ITERS = 3
REACH = 2
F32 = jnp.float32
BF16 = jnp.bfloat16
MESH = pl.DeviceIdType.MESH


def dot(a, b, ca=1, cb=0):
    return lax.dot_general(a, b, (((ca,), (cb,)), ((), ())), preferred_element_type=F32)


def hot(test):
    return jnp.where(test, 1.0, 0.0).astype(BF16)


def layout(d):
    f, b, share, pd, rows = d.f, d.b, d.share, d.pd, d.rows
    exc, dest = d.exc, d.dest
    spots = (2 * REACH + 1) * pd

    def one(kind, *shape):
        return pltpu.VMEM(shape, kind)

    def each(kind, *shape):
        return [one(kind, *shape) for _ in range(ITERS)]

    return dict(
        x=each(BF16, spots, exc, rows),
        psend=each(BF16, pd, exc, rows),
        precv=each(BF16, pd, f - 1, share, rows),
        xface_send=each(BF16, 2, d.cy, d.cz, exc),
        yface_send=each(BF16, 2, d.cx, d.cz, exc),
        xface_recv=each(BF16, 2, d.cy, d.cz, exc),
        yface_recv=each(BF16, 2, d.cx, d.cz, exc),
        out_send=each(BF16, b, CAP, exc),
        out_recv=each(BF16, b, CAP, exc),
        val_send=each(BF16, b, CAP, exc),
        val_recv=each(BF16, b, CAP, exc),
        red_send=each(BF16, share, 128),
        red_recv=each(BF16, b, share, 128),
        fem=[one(F32, d.cx + 2, d.cy + 2, d.cz, exc) for _ in range(2)],
        acc=one(F32, pd, exc, rows),
        den=one(F32, pd, share, rows),
        row_send=one(F32, b, CAP, 128),
        row_recv=one(F32, b, CAP, 128),
        load=one(F32, d.cx, d.cy, d.cz, exc),
        inv=one(F32, d.cx, d.cy, d.cz, exc),
        whole=one(F32, exc, pd * rows),
        bsrc=one(F32, share, pd * rows),
        blocks=one(BF16, pd, d.group, rows, rows),
        pick_cell=one(BF16, d.cx, dest, d.cy * d.cz),
        put_cell=one(BF16, d.cx, d.cy * d.cz, dest),
        pick_row=one(BF16, dest, pd * rows),
        right=one(BF16, pd, d.rank, rows),
        right_wide=one(BF16, pd, 128, rows),
        left_wide=one(BF16, pd, 128, rows),
        traced=one(F32, exc, pd * rows),
        base=one(F32, share, pd * rows),
        bank=one(jnp.int32, 1, d.slots),
        node=one(jnp.int32, 1, d.slots),
        cell=one(jnp.int32, 1, d.slots),
        pairs=one(jnp.int32, pd, d.pairs),
        centers=one(F32, 3, b * pd),
        reaction=one(F32, d.cx, d.cy, d.cz),
        diag=one(F32, 1, pd * rows),
        left=one(BF16, pd, d.rank, rows),
        kernel=one(F32, pd, b * pd, 128),
    )


def solve_kernel(
    d,
    pairs_ref,
    bank_hbm,
    node_hbm,
    cell_hbm,
    pairs_hbm,
    centers_hbm,
    reaction_hbm,
    diag_hbm,
    left_hbm,
    fem_hbm,
    load_hbm,
    density_hbm,
    bsrc_hbm,
    blocks_hbm,
    right_hbm,
    fem_out,
    bem_out,
    *scratch,
):
    places = jax.tree.structure(layout(d))
    r = Dims(**jax.tree.unflatten(places, scratch[:-3]))
    send_sem, recv_sem, load_sem = scratch[-3:]
    F, B, pd, share, rows, exc = d.f, d.b, d.pd, d.share, d.rows, d.exc
    f, b = lax.axis_index("fem"), lax.axis_index("bem")
    odd = lax.rem(b, 2)
    home = REACH * pd
    arrivals, loads = iter(range(recv_sem.shape[0])), iter(range(load_sem.shape[0]))
    senders, leaving = {}, {}

    def sender(key):
        if key in leaving:
            leaving.pop(key)()
        slot = senders.setdefault(key, len(senders))
        assert slot < send_sem.shape[0]
        return send_sem.at[slot]

    def fem_peer(step):
        return (lax.rem(f + step + F, F), b)

    def flipped(flips):
        index = 0
        for i in range((F - 1).bit_length()):
            bit = lax.rem(f // (1 << i), 2)
            index += (1 - bit if flips >> i & 1 else bit) * (1 << i)
        return index

    def across_fem(flips):
        return (flipped(flips), b)

    def bem_peer(step):
        return (f, lax.rem(b + step + B, B))

    def remote(src, dst, place, ssem, rsem):
        return pltpu.make_async_remote_copy(
            src_ref=src,
            dst_ref=dst,
            send_sem=ssem,
            recv_sem=rsem,
            device_id=place,
            device_id_type=MESH,
        )

    def send(src, dst, place, key):
        copy = remote(src, dst, place, sender(key), recv_sem.at[next(arrivals)])
        copy.start()
        leaving[key] = copy.wait_send
        return copy.wait_recv

    def send_fem(src_of, dst_of, flips, size_ref, key):
        ssem, rsem = sender(key), recv_sem.at[next(arrivals)]
        for k in flips:
            remote(src_of(k), dst_of(k), across_fem(k), ssem, rsem).start()
        leaving[key] = pltpu.make_async_copy(size_ref, size_ref, ssem).wait
        return pltpu.make_async_copy(size_ref, size_ref, rsem).wait

    def fetch(src, dst):
        copy = pltpu.make_async_copy(src, dst, load_sem.at[next(loads)])
        copy.start()
        return copy

    opposite = F - 1
    nearby = range(1, F - 1)

    def spread(src_of, dst_ref, sign, key):
        ssem, rsem = sender(key), recv_sem.at[next(arrivals)]
        for s in range(1, B):
            remote(src_of(s), dst_ref.at[s], bem_peer(sign * s), ssem, rsem).start()
        rest = dst_ref.at[1:]
        leaving[key] = pltpu.make_async_copy(rest, rest, ssem).wait
        return pltpu.make_async_copy(rest, rest, rsem).wait

    whole_in = fetch(density_hbm, r.whole)
    small_in = [
        fetch(bank_hbm, r.bank),
        fetch(node_hbm, r.node),
        fetch(cell_hbm, r.cell),
    ]
    first = fetch(fem_hbm, r.fem[0].at[1 : d.cx + 1, 1 : d.cy + 1])
    right_in = fetch(right_hbm.at[pl.ds(b * pd, pd)], r.right)
    bsrc_in = fetch(bsrc_hbm.at[pl.ds(pl.multiple_of(f * share, share), share)], r.bsrc)
    load_in = fetch(load_hbm, r.load)
    other_in = [
        fetch(pairs_hbm, r.pairs),
        fetch(centers_hbm, r.centers),
        fetch(reaction_hbm, r.reaction),
        fetch(diag_hbm, r.diag),
        fetch(left_hbm, r.left),
        bsrc_in,
        load_in,
    ]

    barrier = pltpu.get_barrier_semaphore()
    for s in range(1, F):
        pl.semaphore_signal(barrier, inc=1, device_id=fem_peer(s), device_id_type=MESH)
    for s in range(1, B):
        pl.semaphore_signal(barrier, inc=1, device_id=bem_peer(s), device_id_type=MESH)
    blocks_in = [fetch(blocks_hbm.at[p], r.blocks.at[p]) for p in range(pd)]

    whole_in.wait()
    for p in range(pd):
        cols = slice(p * rows, (p + 1) * rows)
        r.x[0][home + p] = r.whole[:, cols].astype(BF16)
        r.den[p] = r.whole[pl.ds(pl.multiple_of(f * share, share), share), cols]
    pl.semaphore_wait(barrier, F - 1 + B - 1)

    def rows_of(index):
        return pl.ds(pl.multiple_of(index * share, share), share)

    own_rows, opposite_rows = rows_of(f), rows_of(flipped(opposite))
    state = Dims(
        faces={},
        fwd={},
        homes={},
        out={},
        own={},
        turned={},
        parts={},
        red={},
        sides={},
        val={},
        z={},
    )

    def partner_copy(n, p, which):
        x = r.x[n]
        if which == "home":
            there = jnp.where(odd == 0, -1, 1)
            source = home + p
        else:
            there = jnp.where(odd == 0, 1, -1)
            source = (REACH + 2 * there) * pd + p
        target = (REACH + there) * pd + p
        place = (f, b + 1 - 2 * odd)
        return send(x.at[pl.ds(source, 1)], x.at[pl.ds(target, 1)], place, (which, p))

    def along_bem(n, p, span, key):
        x = r.x[n]
        return {
            side: send(
                x.at[home + p, span],
                x.at[(REACH - side) * pd + p, span],
                bem_peer(side),
                (key, p, side),
            )
            for side in (2, -2)
        }

    def start_share(n, p):
        mine = r.x[n].at[home + p, own_rows]
        state.z[n, p] = along_bem(n, p, own_rows, "z")
        if n > 0:
            size = r.precv[n].at[p]
            state.own[n, p] = [
                send_fem(
                    lambda k: mine, lambda k: mine, flips, size.at[0 : len(flips)], (tag, p)
                )
                for tag, flips in (("far", (opposite,)), ("own", nearby))
            ]

    def turn(n, p):
        if n > 0:
            state.own[n, p][0]()
        state.turned[n, p] = along_bem(n, p, opposite_rows, "m")

    def forward(n, p):
        state.fwd[n, p] = []
        for side in (2, -2):
            state.z[n, p][side]()
            piece = r.x[n].at[(REACH - side) * pd + p, own_rows]
            size = r.precv[n].at[p, 0 : len(nearby)]
            state.fwd[n, p].append(
                send_fem(
                    lambda k: piece, lambda k: piece, nearby, size, ("fwd", p, side)
                )
            )

    def homes(n, p):
        if n > 0:
            state.own[n, p][1]()
        state.homes[n, p] = partner_copy(n, p, "home")

    def sides(n, p):
        for arrive in (*state.turned[n, p].values(), *state.fwd[n, p]):
            arrive()
        state.sides[n, p] = partner_copy(n, p, "sides")

    def reduce_own(n):
        total = 0.0
        for p in range(pd):
            mine = r.x[n][home + p, own_rows, :]
            total += dot(mine, r.right_wide[p], 1, 1)
        r.red_send[n][...] = total.astype(BF16)
        r.red_recv[n][0] = total.astype(BF16)
        state.red[n] = spread(lambda s: r.red_send[n], r.red_recv[n], 1, "red")

    def send_picked(n, acc):
        out = acc.astype(BF16).reshape(B, CAP, exc)
        r.out_send[n][...] = out
        r.out_recv[n][0] = out[0]
        state.out[n] = spread(lambda s: r.out_send[n].at[s], r.out_recv[n], 1, "out")

    def send_faces(n):
        fem = r.fem[n % 2]
        xs, ys = r.xface_send[n], r.yface_send[n]
        xr, yr = r.xface_recv[n], r.yface_recv[n]
        xs[0] = fem[d.cx, 1 : d.cy + 1].astype(BF16)
        xs[1] = fem[1, 1 : d.cy + 1].astype(BF16)
        ys[0] = fem[1 : d.cx + 1, d.cy].astype(BF16)
        ys[1] = fem[1 : d.cx + 1, 1].astype(BF16)
        waits = []
        for out, got, rank, size, peer in ((xs, xr, f, F, fem_peer), (ys, yr, b, B, bem_peer)):
            for i, step in enumerate((1, -1)):
                goes = rank < size - 1 if step == 1 else rank > 0
                comes = rank > 0 if step == 1 else rank < size - 1
                key = ("face", len(waits))
                copy = remote(out.at[i], got.at[i], peer(step), sender(key), recv_sem.at[next(arrivals)])
                pl.when(goes)(copy.start)
                leaving[key] = functools.partial(pl.when(goes), copy.wait_send)
                waits.append((comes, copy))
        state.faces[n] = waits

    def take_faces(n):
        fem = r.fem[n % 2]
        xr, yr = r.xface_recv[n], r.yface_recv[n]

        def put(i):
            if i == 0:
                fem[0, 1 : d.cy + 1] = xr[0].astype(F32)
            elif i == 1:
                fem[d.cx + 1, 1 : d.cy + 1] = xr[1].astype(F32)
            elif i == 2:
                fem[1 : d.cx + 1, 0] = yr[0].astype(F32)
            else:
                fem[1 : d.cx + 1, d.cy + 1] = yr[1].astype(F32)

        def clear(i):
            if i < 2:
                fem[(0, d.cx + 1)[i], 1 : d.cy + 1] = jnp.zeros((d.cy, d.cz, exc), F32)
            else:
                fem[1 : d.cx + 1, (0, d.cy + 1)[i - 2]] = jnp.zeros((d.cx, d.cz, exc), F32)

        for i, (comes, copy) in enumerate(state.faces[n]):

            def take(i=i, copy=copy):
                copy.wait_recv()
                put(i)

            pl.when(comes)(take)
            pl.when(jnp.logical_not(comes))(functools.partial(clear, i))

    def picked_first():
        def body(x, acc):
            plane = r.fem[0][x + 1, 1 : d.cy + 1].astype(BF16).reshape(d.cy * d.cz, exc)
            return acc + dot(r.pick_cell[x], plane)

        return lax.fori_loop(0, d.cx, body, jnp.zeros((d.dest, exc), F32))

    def fem_step(n):
        take_faces(n)
        state.val[n]()
        last = n == ITERS - 1
        old, fresh = r.fem[n % 2], r.fem[(n + 1) % 2]
        values = r.val_recv[n][...].reshape(d.dest, exc)
        level = lax.broadcasted_iota(jnp.int32, (d.cy, d.cz, exc), 1)

        def body(x, acc):
            coupled = dot(r.put_cell[x], values).reshape(d.cy, d.cz, exc)
            here = old[x + 1, 1 : d.cy + 1]
            beside = old[x, 1 : d.cy + 1] + old[x + 2, 1 : d.cy + 1]
            beside += old[x + 1, 0 : d.cy] + old[x + 1, 2 : d.cy + 2]
            beside += jnp.where(level > 0, pltpu.roll(here, 1, 1), 0.0)
            beside += jnp.where(level < d.cz - 1, pltpu.roll(here, d.cz - 1, 1), 0.0)
            result = (r.load[x] + beside - coupled) * r.inv[x]
            if last:
                fem_out[x] = result
                return acc
            fresh[x + 1, 1 : d.cy + 1] = result
            plane = result.astype(BF16).reshape(d.cy * d.cz, exc)
            return acc + dot(r.pick_cell[x], plane)

        acc = lax.fori_loop(0, d.cx, body, jnp.zeros((8 if last else d.dest, exc), F32))
        if not last:
            send_picked(n + 1, acc)

    def trace_values(n):
        values = 0.0
        for p in range(pd):
            values += dot(r.pick_row[:, p * rows : (p + 1) * rows], r.x[n][home + p], 1, 1)
        out = values.astype(BF16).reshape(B, CAP, exc)
        r.val_send[n][...] = out
        r.val_recv[n][0] = out[0]
        state.val[n] = spread(lambda s: r.val_send[n].at[s], r.val_recv[n], -1, "val")

    def trace_fem(n):
        state.out[n]()
        incoming = r.out_recv[n][...].reshape(d.dest, exc)
        r.traced[...] = dot(incoming, r.pick_row[...], 0, 0)

    def far(n):
        state.red[n]()
        for p in range(pd):
            total = jnp.zeros((share, 128), F32)
            for s in range(B):
                scale = jnp.zeros((1, 128), F32)
                for q in range(pd):
                    at = lax.rem(b - s + B, B) * pd + q
                    group = (lane128 >= q * d.rank) & (lane128 < (q + 1) * d.rank)
                    scale = jnp.where(group, r.kernel[p, pl.ds(at, 1), :], scale)
                total += r.red_recv[n][s].astype(F32) * scale
            high = total.astype(BF16)
            low = (total - high.astype(F32)).astype(BF16)
            distant = dot(high, r.left_wide[p]) + dot(low, r.left_wide[p])
            cols = slice(p * rows, (p + 1) * rows)
            r.base[:, cols] = r.bsrc[:, cols] - distant

    def near(n):
        for p in range(pd):
            state.sides[n, p]()
            state.homes[n, p]()
        x = r.x[n]
        for p in range(pd):
            cols = slice(p * rows, (p + 1) * rows)
            acc = r.traced[:, cols]
            for k in range(d.group):
                pair = pairs_ref[p, f * d.group + k]
                spot = lax.rem(pair - b * pd + REACH * pd + B * pd, B * pd)
                spot = jnp.minimum(spot, (2 * REACH + 1) * pd - 1)
                acc += dot(x[spot], r.blocks[p, k])
            r.acc[p] = acc
            out, got = r.psend[n], r.precv[n]
            out[p] = acc.astype(BF16)
            state.parts[n, p] = send_fem(
                lambda k: out.at[p, rows_of(flipped(k))],
                lambda k: got.at[p, k - 1],
                range(F - 1, 0, -1),
                got.at[p],
                ("part", p),
            )

    def update(n, p):
        state.parts[n, p]()
        last = n == ITERS - 1
        cols = slice(p * rows, (p + 1) * rows)
        total = r.acc[p, own_rows, :]
        for k in range(F - 1):
            total += r.precv[n][p, k].astype(F32)
        fresh = r.den[p] + (r.base[:, cols] - total) / r.diag[:, cols]
        if last:
            bem_out[:, cols] = fresh
        else:
            r.den[p] = fresh
            r.x[n + 1][home + p, own_rows, :] = fresh.astype(BF16)
            start_share(n + 1, p)

    for p in range(pd):
        start_share(0, p)
    for p in range(pd):
        turn(0, p)
        homes(0, p)

    def column(row):
        size = row.shape[1]
        down = lax.broadcasted_iota(jnp.int32, (size, size), 0)
        across = lax.broadcasted_iota(jnp.int32, (size, size), 1)
        return jnp.sum(jnp.where(down == across, row, 0.0), axis=1, keepdims=True)

    count, dest = d.slots, d.dest
    lane128 = lax.broadcasted_iota(jnp.int32, (1, 128), 1)
    for copy in small_in:
        copy.wait()
    node_row = r.node[...].astype(F32)
    cell_row = r.cell[...].astype(F32)
    step_row = lax.rem(r.bank[...] - b + B, B).astype(F32)
    down = lax.broadcasted_iota(jnp.int32, (count, count), 0)
    across = lax.broadcasted_iota(jnp.int32, (count, count), 1)
    earlier = (column(step_row) == step_row) & (down < across)
    order = jnp.sum(jnp.where(earlier, 1.0, 0.0), axis=0, keepdims=True)
    target = step_row * CAP + order
    lands = lax.broadcasted_iota(jnp.int32, (dest, count), 0).astype(F32) == target
    row_col = jnp.sum(jnp.where(lands, node_row + 1.0, 0.0), axis=1, keepdims=True) - 1.0
    cell_col = jnp.sum(jnp.where(lands, cell_row + 1.0, 0.0), axis=1, keepdims=True) - 1.0
    row_wide = jnp.broadcast_to(row_col, (dest, 128)).reshape(B, CAP, 128)
    r.row_send[...] = row_wide
    r.row_recv[0] = row_wide[0]
    row_in = spread(lambda s: r.row_send.at[s], r.row_recv, 1, "row")

    right_in.wait()
    for p in range(pd):
        r.right_wide[p] = jnp.zeros((128, rows), BF16)
        r.right_wide[p, p * d.rank : (p + 1) * d.rank, :] = r.right[p]
    reduce_own(0)

    plane = d.cy * d.cz
    ids_lane = lax.broadcasted_iota(jnp.int32, (dest, plane), 1).astype(F32)
    for x in range(d.cx):
        r.pick_cell[x] = hot(cell_col - float(x * plane) == ids_lane)
    first.wait()
    send_picked(0, picked_first())
    for p in range(pd):
        forward(0, p)
    send_faces(0)

    lands_t = lax.broadcasted_iota(jnp.int32, (count, dest), 1).astype(F32) == column(target)
    cell_send = (
        jnp.sum(jnp.where(lands_t, column(cell_row) + 1.0, 0.0), axis=0, keepdims=True) - 1.0
    )
    ids_down = lax.broadcasted_iota(jnp.int32, (plane, dest), 0).astype(F32)
    for x in range(d.cx):
        r.put_cell[x] = hot(cell_send - float(x * plane) == ids_down)

    for copy in other_in:
        copy.wait()
    for p in range(pd):
        r.left_wide[p] = jnp.zeros((128, rows), BF16)
        for q in range(pd):
            r.left_wide[p, q * d.rank : (q + 1) * d.rank, :] = r.left[p]
    total = B * pd
    panel_row = lax.broadcasted_iota(jnp.int32, (1, total), 1)
    panel_col = lax.broadcasted_iota(jnp.int32, (total, 1), 0)
    for p in range(pd):
        own = b * pd + p
        square = jnp.zeros((total, 1), F32)
        for i in range(3):
            place = r.centers[i : i + 1, :]
            mine = jnp.sum(jnp.where(panel_row == own, place, 0.0), axis=1, keepdims=True)
            apart = mine - column(place)
            square += apart * apart
        named = jnp.where(r.pairs[p : p + 1, :] == panel_col, 1.0, 0.0)
        listed = jnp.max(named, axis=1, keepdims=True) + jnp.where(panel_col == own, 1.0, 0.0)
        weight = jnp.where(listed > 0.0, 0.0, 1.0 / (1.0 + square))
        r.kernel[p] = jnp.broadcast_to(weight, (total, 128))

    def spread_inverse(x, carry):
        inverse = 1.0 / (6.0 + r.reaction[x])
        for y in range(d.cy):
            wide = jnp.broadcast_to(column(inverse[y : y + 1, :]), (d.cz, exc))
            r.inv[x, y] = wide
        return carry

    lax.fori_loop(0, d.cx, spread_inverse, 0)

    for n in range(ITERS):
        last = n == ITERS - 1
        if n > 0:
            reduce_own(n)
            fem_step(n - 1)
            for p in range(pd):
                turn(n, p)
                forward(n, p)
            send_faces(n)
            for p in range(pd):
                homes(n, p)
        if n == 0:
            row_in()
            wanted = r.row_recv[...].reshape(dest, 128)
            lanes = lax.broadcasted_iota(jnp.int32, (dest, 128), 1).astype(F32)
            for j in range(pd * rows // 128):
                r.pick_row[:, j * 128 : (j + 1) * 128] = hot(wanted - float(j * 128) == lanes)
        trace_values(n)
        trace_fem(n)
        far(n)
        if n == 0:
            for copy in blocks_in:
                copy.wait()
        for p in range(pd):
            sides(n, p)
        near(n)
        if last:
            fem_step(n)
        for p in range(pd):
            update(n, p)

    for finish in leaving.values():
        finish()


def hand_over(fem_in, bem_in, fem_out, bem_out, out_sem):
    moves = ((fem_in, fem_out), (bem_in, bem_out))
    outs = [pltpu.make_async_copy(m, o, out_sem.at[i]) for i, (m, o) in enumerate(moves)]
    for copy in outs:
        copy.start()
    for copy in outs:
        copy.wait()


class Dims:
    def __init__(self, **items):
        self.__dict__.update(items)


def shards(
    fem_field,
    fem_source,
    reaction,
    bem_density,
    bem_source,
    bem_diagonal,
    near_blocks,
    near_pairs,
    low_left,
    low_right,
    centers,
    trace_cell,
    trace_bank,
    trace_row,
):
    d = Dims()
    d.f, d.b = lax.axis_size("fem"), lax.axis_size("bem")
    d.pd, d.group, d.rows, _ = near_blocks.shape
    d.rank = low_right.shape[1]
    d.cx, d.cy, d.cz, d.exc = fem_field.shape
    d.share = d.exc // d.f
    d.slots = trace_cell.shape[0]
    d.dest = d.b * CAP
    d.pairs = near_pairs.shape[1]

    items = jax.tree.leaves(layout(d))
    vmem = pl.BlockSpec(memory_space=pltpu.VMEM)
    far_off = pl.BlockSpec(memory_space=pltpu.HBM)
    results = pl.pallas_call(
        functools.partial(solve_kernel, d),
        out_shape=[
            pltpu.VMEM(fem_field.shape, F32),
            pltpu.VMEM((d.share, d.pd * d.rows), F32),
        ],
        in_specs=[pl.BlockSpec(memory_space=pltpu.SMEM)] + [far_off] * 14,
        out_specs=[vmem, vmem],
        scratch_shapes=items
        + [
            pltpu.SemaphoreType.DMA((30,)),
            pltpu.SemaphoreType.DMA((84,)),
            pltpu.SemaphoreType.DMA((17,)),
        ],
        cost_estimate=pl.CostEstimate(flops=1 << 33, bytes_accessed=1 << 24, transcendentals=0),
        compiler_params=pltpu.CompilerParams(
            collective_id=0, has_side_effects=True, vmem_limit_bytes=54 << 20
        ),
        name="sweeps",
    )(
        near_pairs,
        trace_bank.reshape(1, d.slots),
        trace_row[None, :],
        trace_cell[None, :],
        near_pairs,
        centers.T,
        reaction,
        bem_diagonal[None, :],
        low_left,
        fem_field,
        fem_source,
        bem_density,
        bem_source,
        near_blocks,
        low_right,
    )
    return pl.pallas_call(
        hand_over,
        out_shape=[jax.ShapeDtypeStruct(x.shape, x.dtype) for x in results],
        in_specs=[vmem] * 2,
        out_specs=[far_off] * 2,
        scratch_shapes=[pltpu.SemaphoreType.DMA((2,))],
        compiler_params=pltpu.CompilerParams(vmem_limit_bytes=4 << 20),
        name="hand_over",
    )(*results)


def solution(mesh):
    return jax.shard_map(
        shards,
        mesh=mesh,
        in_specs=(
            P("fem", "bem", None, None),
            P("fem", "bem", None, None),
            P("fem", "bem", None),
            P(None, "bem"),
            P(None, "bem"),
            P("bem"),
            P("bem", "fem", None, None),
            P("bem", None),
            P("bem", None, None),
            P(),
            P(),
            P(("fem", "bem")),
            P(("fem", "bem"), None),
            P(("fem", "bem")),
        ),
        out_specs=(P("fem", "bem", None, None), P("fem", "bem")),
        check_vma=False,
    )
```

time: 179 us -> 64.1 us (0.36)
  waiting for transfers between devices: 51.8 us -> 0 us
  Pallas kernels: 93.2 us -> 63.3 us
  between operations: 14.5 us -> 0.64 us
  other arithmetic: 10.2 us -> 0 us
  matrix products: 6.22 us -> 0 us
  local copies, waits for them, and re-layouts: 2.71 us -> 0 us
    all_gather x3 -> x0, waiting for transfers between devices: 51.8 us -> none  [shards(): x = lax.all_gather(narrow, 'bem', axis=0, tiled=True)]
    pallas_call x14 -> x2, Pallas kernels: 93.2 us -> 63.3 us  [the longest x1 62.3 us: shards(): pl.pallas_call(functools.partial(solve_kernel, d), out_shape=[pltpu.VMEM(...]
    dot_general x18 -> x0, matrix products: 6.22 us -> none  [the longest x3 1.46 us: shards(): jnp.dot(send_hot, fem_state.astype(jnp.bfloat16).reshape(cell_total, exci...]
    add x6 -> x0, other arithmetic: 3.8 us -> none  [the longest x1 2.18 us: shards(): fem_state + (fem_source - (scale * fem_state - beside) - coupled) / scale]
    another operation x3 -> x0, other arithmetic: 3.54 us -> none
    convert_element_type x14 -> x0, other arithmetic: 2.17 us -> none  [the longest x2 1.97 us: shards(): narrow = whole.astype(jnp.bfloat16).reshape(-1, local_panels, panel_rows)]
  transfers between devices with their start and end apart: 3 -> 0, of which waited for: 3 -> 0; matrix products, arithmetic and copies ran while one was open for 5% -> 0% of each run, Pallas kernels for 18% -> 0%
where the time goes in v1:
time: 64.1 us; the launch traced here: 63.9 us
  Pallas kernels  63.3 us (99%)
    pallas_call x1, Pallas kernels, shards(): pl.pallas_call(functools.partial(solve_kernel, d), out_shape=[pltpu.VMEM(...  62.3 us

profile of v1, /device:TPU:0, one launch (start us, length us, event | category | flops | bytes accessed | tf_op | source)
XLA Modules:
  0.0 63.9 jit_solution(3733268775493064773)
XLA Ops:
  0.6 62.3 %sweeps.1 = (f32[8,8,32,128]{3,2,1,0:T(8,128)S(1)}, f32[32,1024]{1,0:T(8,128)S(1)}) custom-call(s32[2,48]{1,0:T(2,128)} %pairs_hbm.1, s32[1,256]{1,0:T(1,128)} %bitcast.7, s32[1,256]{1,0:T(1,128)} %bitcast.8, s32[1,256]{1,0:T(1,128)} %bitcast.9, s32[2,48]{1,0:T(2,128)} %pairs_hbm.1, f32[3,16]{1,0:T(4,128)} %bitcast.6, f32[8,8,32]{2,1,0:T(8,128)} %reaction_hbm.1, ...), custom_call_target="tpu_custom_call" | custom-call | flops 8589934592 | bytes 16777216 | tf_op jit(solution)/shard_map/sweeps/pallas_call | solution.py:622
  62.9 1.0 %hand_over.1 = (f32[8,8,32,128]{3,2,1,0:T(8,128)}, f32[32,1024]{1,0:T(8,128)}) custom-call(f32[8,8,32,128]{3,2,1,0:T(8,128)S(1)} %get-tuple-element.4.fem_in, f32[32,1024]{1,0:T(8,128)S(1)} %get-tuple-element.5.bem_in), custom_call_target="tpu_custom_call" | custom-call | tf_op jit(solution)/shard_map/hand_over/pallas_call | solution.py:658

commit v2 on v1

--- a/solution.py
+++ b/solution.py
@@ -46,13 +46,13 @@
         out_recv=each(BF16, b, CAP, exc),
         val_send=each(BF16, b, CAP, exc),
         val_recv=each(BF16, b, CAP, exc),
-        red_send=each(BF16, share, 128),
-        red_recv=each(BF16, b, share, 128),
+        red_send=each(BF16, share // 2, 128),
+        red_recv=each(BF16, b, share // 2, 128),
         fem=[one(F32, d.cx + 2, d.cy + 2, d.cz, exc) for _ in range(2)],
         acc=one(F32, pd, exc, rows),
         den=one(F32, pd, share, rows),
-        row_send=one(F32, b, CAP, 128),
-        row_recv=one(F32, b, CAP, 128),
+        row_send=one(F32, 1, dest),
+        row_recv=one(F32, b, 1, dest),
         load=one(F32, d.cx, d.cy, d.cz, exc),
         inv=one(F32, d.cx, d.cy, d.cz, exc),
         whole=one(F32, exc, pd * rows),
@@ -291,8 +291,9 @@
         for p in range(pd):
             mine = r.x[n][home + p, own_rows, :]
             total += dot(mine, r.right_wide[p], 1, 1)
-        r.red_send[n][...] = total.astype(BF16)
-        r.red_recv[n][0] = total.astype(BF16)
+        folded = (total[: share // 2] + pltpu.roll(total[share // 2 :], 64, 1)).astype(BF16)
+        r.red_send[n][...] = folded
+        r.red_recv[n][0] = folded
         state.red[n] = spread(lambda s: r.red_send[n], r.red_recv[n], 1, "red")
 
     def send_picked(n, acc):
@@ -401,14 +402,17 @@
     def far(n):
         state.red[n]()
         for p in range(pd):
-            total = jnp.zeros((share, 128), F32)
+            total = jnp.zeros((share // 2, 128), F32)
             for s in range(B):
                 scale = jnp.zeros((1, 128), F32)
                 for q in range(pd):
                     at = lax.rem(b - s + B, B) * pd + q
-                    group = (lane128 >= q * d.rank) & (lane128 < (q + 1) * d.rank)
+                    group = (lane64 >= q * d.rank) & (lane64 < (q + 1) * d.rank)
                     scale = jnp.where(group, r.kernel[p, pl.ds(at, 1), :], scale)
                 total += r.red_recv[n][s].astype(F32) * scale
+            first = jnp.where(lane128 < 64, total, 0.0)
+            second = jnp.where(lane128 < 64, pltpu.roll(total, 64, 1), 0.0)
+            total = jnp.concatenate([first, second], axis=0)
             high = total.astype(BF16)
             low = (total - high.astype(F32)).astype(BF16)
             distant = dot(high, r.left_wide[p]) + dot(low, r.left_wide[p])
@@ -468,6 +472,7 @@
 
     count, dest = d.slots, d.dest
     lane128 = lax.broadcasted_iota(jnp.int32, (1, 128), 1)
+    lane64 = lax.rem(lane128, 64)
     for copy in small_in:
         copy.wait()
     node_row = r.node[...].astype(F32)
@@ -479,12 +484,17 @@
     order = jnp.sum(jnp.where(earlier, 1.0, 0.0), axis=0, keepdims=True)
     target = step_row * CAP + order
     lands = lax.broadcasted_iota(jnp.int32, (dest, count), 0).astype(F32) == target
-    row_col = jnp.sum(jnp.where(lands, node_row + 1.0, 0.0), axis=1, keepdims=True) - 1.0
     cell_col = jnp.sum(jnp.where(lands, cell_row + 1.0, 0.0), axis=1, keepdims=True) - 1.0
-    row_wide = jnp.broadcast_to(row_col, (dest, 128)).reshape(B, CAP, 128)
-    r.row_send[...] = row_wide
-    r.row_recv[0] = row_wide[0]
-    row_in = spread(lambda s: r.row_send.at[s], r.row_recv, 1, "row")
+    lands_t = lax.broadcasted_iota(jnp.int32, (count, dest), 1).astype(F32) == column(target)
+    row_lane = (
+        jnp.sum(jnp.where(lands_t, column(node_row) + 1.0, 0.0), axis=0, keepdims=True) - 1.0
+    )
+    r.row_send[...] = row_lane
+    r.row_recv[0] = row_lane
+    row_in = spread(lambda s: r.row_send, r.row_recv, 1, "row")
+
+    for p in range(pd):
+        forward(0, p)
 
     right_in.wait()
     for p in range(pd):
@@ -498,77 +508,85 @@
         r.pick_cell[x] = hot(cell_col - float(x * plane) == ids_lane)
     first.wait()
     send_picked(0, picked_first())
-    for p in range(pd):
-        forward(0, p)
     send_faces(0)
 
-    lands_t = lax.broadcasted_iota(jnp.int32, (count, dest), 1).astype(F32) == column(target)
-    cell_send = (
-        jnp.sum(jnp.where(lands_t, column(cell_row) + 1.0, 0.0), axis=0, keepdims=True) - 1.0
-    )
-    ids_down = lax.broadcasted_iota(jnp.int32, (plane, dest), 0).astype(F32)
-    for x in range(d.cx):
-        r.put_cell[x] = hot(cell_send - float(x * plane) == ids_down)
-
-    for copy in other_in:
-        copy.wait()
-    for p in range(pd):
-        r.left_wide[p] = jnp.zeros((128, rows), BF16)
-        for q in range(pd):
-            r.left_wide[p, q * d.rank : (q + 1) * d.rank, :] = r.left[p]
-    total = B * pd
-    panel_row = lax.broadcasted_iota(jnp.int32, (1, total), 1)
-    panel_col = lax.broadcasted_iota(jnp.int32, (total, 1), 0)
-    for p in range(pd):
-        own = b * pd + p
-        square = jnp.zeros((total, 1), F32)
-        for i in range(3):
-            place = r.centers[i : i + 1, :]
-            mine = jnp.sum(jnp.where(panel_row == own, place, 0.0), axis=1, keepdims=True)
-            apart = mine - column(place)
-            square += apart * apart
-        named = jnp.where(r.pairs[p : p + 1, :] == panel_col, 1.0, 0.0)
-        listed = jnp.max(named, axis=1, keepdims=True) + jnp.where(panel_col == own, 1.0, 0.0)
-        weight = jnp.where(listed > 0.0, 0.0, 1.0 / (1.0 + square))
-        r.kernel[p] = jnp.broadcast_to(weight, (total, 128))
-
-    def spread_inverse(x, carry):
-        inverse = 1.0 / (6.0 + r.reaction[x])
-        for y in range(d.cy):
-            wide = jnp.broadcast_to(column(inverse[y : y + 1, :]), (d.cz, exc))
-            r.inv[x, y] = wide
-        return carry
-
-    lax.fori_loop(0, d.cx, spread_inverse, 0)
+    def weights_setup():
+        for copy in other_in:
+            copy.wait()
+        for p in range(pd):
+            r.left_wide[p] = jnp.zeros((128, rows), BF16)
+            for q in range(pd):
+                r.left_wide[p, q * d.rank : (q + 1) * d.rank, :] = r.left[p]
+        total = B * pd
+        panel_row = lax.broadcasted_iota(jnp.int32, (1, total), 1)
+        panel_col = lax.broadcasted_iota(jnp.int32, (total, 1), 0)
+        for p in range(pd):
+            own = b * pd + p
+            square = jnp.zeros((total, 1), F32)
+            for i in range(3):
+                place = r.centers[i : i + 1, :]
+                mine = jnp.sum(jnp.where(panel_row == own, place, 0.0), axis=1, keepdims=True)
+                apart = mine - column(place)
+                square += apart * apart
+            named = jnp.where(r.pairs[p : p + 1, :] == panel_col, 1.0, 0.0)
+            listed = jnp.max(named, axis=1, keepdims=True) + jnp.where(panel_col == own, 1.0, 0.0)
+            weight = jnp.where(listed > 0.0, 0.0, 1.0 / (1.0 + square))
+            r.kernel[p] = jnp.broadcast_to(weight, (total, 128))
+
+    def finish_setup():
+        cell_send = (
+            jnp.sum(jnp.where(lands_t, column(cell_row) + 1.0, 0.0), axis=0, keepdims=True) - 1.0
+        )
+        ids_down = lax.broadcasted_iota(jnp.int32, (plane, dest), 0).astype(F32)
+        for x in range(d.cx):
+            r.put_cell[x] = hot(cell_send - float(x * plane) == ids_down)
+
+        def spread_inverse(x, carry):
+            inverse = 1.0 / (6.0 + r.reaction[x])
+            for y in range(d.cy):
+                wide = jnp.broadcast_to(column(inverse[y : y + 1, :]), (d.cz, exc))
+                r.inv[x, y] = wide
+            return carry
+
+        lax.fori_loop(0, d.cx, spread_inverse, 0)
 
     for n in range(ITERS):
         last = n == ITERS - 1
         if n > 0:
             reduce_own(n)
-            fem_step(n - 1)
             for p in range(pd):
                 turn(n, p)
                 forward(n, p)
             send_faces(n)
             for p in range(pd):
                 homes(n, p)
-        if n == 0:
-            row_in()
-            wanted = r.row_recv[...].reshape(dest, 128)
-            lanes = lax.broadcasted_iota(jnp.int32, (dest, 128), 1).astype(F32)
-            for j in range(pd * rows // 128):
-                r.pick_row[:, j * 128 : (j + 1) * 128] = hot(wanted - float(j * 128) == lanes)
-        trace_values(n)
-        trace_fem(n)
-        far(n)
+        if n > 0:
+            trace_values(n)
+            far(n)
         if n == 0:
             for copy in blocks_in:
                 copy.wait()
         for p in range(pd):
             sides(n, p)
+        if n == 0:
+            weights_setup()
+            row_in()
+            lanes = lax.broadcasted_iota(jnp.int32, (CAP, 128), 1).astype(F32)
+            place_down = lax.broadcasted_iota(jnp.int32, (CAP, dest), 0)
+            place_lane = lax.broadcasted_iota(jnp.int32, (CAP, dest), 1)
+            for s in range(B):
+                meant = place_lane == place_down + s * CAP
+                wanted = jnp.sum(jnp.where(meant, r.row_recv[s], 0.0), axis=1, keepdims=True)
+                for j in range(pd * rows // 128):
+                    r.pick_row[s * CAP : (s + 1) * CAP, j * 128 : (j + 1) * 128] = hot(
+                        wanted - float(j * 128) == lanes
+                    )
+            trace_values(n)
+            far(n)
+            finish_setup()
+        trace_fem(n)
         near(n)
-        if last:
-            fem_step(n)
+        fem_step(n)
         for p in range(pd):
             update(n, p)
 
@@ -615,6 +633,7 @@
     d.slots = trace_cell.shape[0]
     d.dest = d.b * CAP
     d.pairs = near_pairs.shape[1]
+    assert d.pd * d.rank <= 64
 
     items = jax.tree.leaves(layout(d))
     vmem = pl.BlockSpec(memory_space=pltpu.VMEM)

time: 64.1 us -> 60.5 us (0.944)
  Pallas kernels: 63.3 us -> 59.7 us
    pallas_call x1, Pallas kernels: 62.3 us -> 58.7 us  [shards(): pl.pallas_call(functools.partial(solve_kernel, d), out_shape=[pltpu.VMEM(...]
where the time goes in v2:
time: 60.5 us; the launch traced here: 60.3 us
  Pallas kernels  59.7 us (99%)
  between operations  0.64 us (1%)
    pallas_call x1, Pallas kernels, shards(): pl.pallas_call(functools.partial(solve_kernel, d), out_shape=[pltpu.VMEM(...  58.7 us

profile of v2, /device:TPU:0, one launch (start us, length us, event | category | flops | bytes accessed | tf_op | source)
XLA Modules:
  0.0 60.3 jit_solution(2827555116987239562)
XLA Ops:
  0.6 58.7 %sweeps.1 = (f32[8,8,32,128]{3,2,1,0:T(8,128)S(1)}, f32[32,1024]{1,0:T(8,128)S(1)}) custom-call(s32[2,48]{1,0:T(2,128)} %pairs_hbm.1, s32[1,256]{1,0:T(1,128)} %bitcast.7, s32[1,256]{1,0:T(1,128)} %bitcast.8, s32[1,256]{1,0:T(1,128)} %bitcast.9, s32[2,48]{1,0:T(2,128)} %pairs_hbm.1, f32[3,16]{1,0:T(4,128)} %bitcast.6, f32[8,8,32]{2,1,0:T(8,128)} %reaction_hbm.1, ...), custom_call_target="tpu_custom_call" | custom-call | flops 8589934592 | bytes 16777216 | tf_op jit(solution)/shard_map/sweeps/pallas_call | solution.py:641
  59.3 1.0 %hand_over.1 = (f32[8,8,32,128]{3,2,1,0:T(8,128)}, f32[32,1024]{1,0:T(8,128)}) custom-call(f32[8,8,32,128]{3,2,1,0:T(8,128)S(1)} %get-tuple-element.4.fem_in, f32[32,1024]{1,0:T(8,128)S(1)} %get-tuple-element.5.bem_in), custom_call_target="tpu_custom_call" | custom-call | tf_op jit(solution)/shard_map/hand_over/pallas_call | solution.py:677
